TPU v7x, 32 devices: a whole 2x2x4 slice. The times are simulated.
32 devices in a mesh: out: 8 (over z, x), inp: 4 (over y, core).
Axes of the slice: x: 2, y: 2, z: 4, core: 2. Of those that a mesh axis runs over, the one named last changes fastest.
Arguments:
- tensor: bfloat16 [1024, 1024, 1024], P('out', 'inp'), may hold values from -0.005859375 to 0.005859375
- state: bfloat16 [768, 1024], P('out'), may hold values from -6 to 6
Outputs:
- collision: bfloat16 [768, 1024], P('inp', 'out')
All inputs are finite; a program needn't handle non-finite values.
Results may differ from a plain program's by a relative error of at most 0.001.
Values may be sent and summed in bfloat16 or wider, within the bound.
A program may use at most 128 MiB of HBM per device.

v0:
```python
import functools

import jax
import jax.numpy as jnp
from jax import lax
from jax.experimental import pallas as pl
from jax.experimental.pallas import tpu as pltpu
from jax.sharding import PartitionSpec as P

MESH = pl.DeviceIdType.MESH
GROUP = 16
SLOTS = 5


def flip(value, bits):
    for bit in (1 << n for n in range(bits.bit_length())):
        if bits & bit:
            value = value + bit * (1 - 2 * ((value // bit) % 2))
    return value


def kernel(nx, n_out, n_inp, tensor, state, out, gathered, turned, chosen, slab, parts, landed,
           z_sems, x_sems, core_sems, t_sems, s_sems, r_sems):
    rows_out, rows_inp, width = tensor.shape
    cells_own = state.shape[0]
    cells = n_out * cells_own
    nz = n_out // nx
    per_owner = n_out // n_inp
    group = slab.shape[1]
    blocks = rows_out // group
    slots = slab.shape[0]
    lanes = 256 if cells % 256 == 0 else cells
    halves = 2
    half_width = width // halves
    early = -(-lanes // cells_own)

    me_o = lax.axis_index("out")
    me_p = lax.axis_index("inp")
    z, x = me_o // nx, me_o % nx
    half = me_p % halves
    partner = me_p + 1 - 2 * half
    cols = pl.ds(pl.multiple_of(half * half_width, 128), half_width)

    def fetch(b, slot):
        return pltpu.make_async_copy(
            tensor.at[pl.ds(b * group, group)], slab.at[slot], t_sems.at[slot])

    for b in range(slots):
        fetch(b, b).start()

    def out_of(d, e):
        return flip(z, d) * nx + flip(x, e)

    barrier = pltpu.get_barrier_semaphore()
    near = [(out_of(d, 0), me_p) for d in range(1, nz)]
    near += [(out_of(0, e), me_p) for e in range(1, nx)]
    near += [(me_o, lax.rem(me_p + q, n_inp)) for q in range(1, n_inp)]
    for device in near:
        pl.semaphore_signal(barrier, inc=1, device_id=device, device_id_type=MESH)
    pl.semaphore_wait(barrier, len(near))

    def remote(src, dst, send, recv, device):
        return pltpu.make_async_remote_copy(
            src_ref=src, dst_ref=dst, send_sem=send, recv_sem=recv,
            device_id=device, device_id_type=MESH)

    def shard(d, e):
        return gathered.at[pl.ds((d * nx + e) * cells_own, cells_own), cols]

    def z_copy(d):
        return remote(state.at[:, cols], shard(d, 0), z_sems.at[0, d], z_sems.at[1, d],
                      (out_of(d, 0), me_p))

    def x_copy(e, d):
        return remote(state.at[:, cols] if d == 0 else shard(d, 0), shard(d, e),
                      x_sems.at[0, e, d], x_sems.at[1, e, d], (out_of(0, e), me_p))

    def core_copy(e, d):
        return remote(shard(d, e), shard(d, e), core_sems.at[0, e, d], core_sems.at[1, e, d],
                      (me_o, partner))

    def relay_x(d):
        for e in range(1, nx):
            x_copy(e, d).wait_recv()
            core_copy(e, d).start()

    def relay_z(d):
        z_copy(d).wait_recv()
        for e in range(1, nx):
            x_copy(e, d).start()
        core_copy(0, d).start()

    for e in range(1, nx):
        x_copy(e, 0).start()
    for d in range(1, nz):
        z_copy(d).start()
    gathered[0:cells_own, :] = state[...]
    relay_x(0)
    relay_z(1)
    order = [(d, e) for d in range(nz) for e in range(nx)]
    for d, e in order[1:early]:
        core_copy(e, d).wait_recv()

    first = pl.multiple_of(me_p * rows_inp, rows_inp)

    def turn(start, stop):
        for j in range(0, width, 128):
            turned[j:j + 128, start:stop] = gathered[start:stop, j:j + 128].T
        chosen[:, start:stop] = turned[pl.ds(first, rows_inp), start:stop].astype(jnp.float32)

    def send_part(b, q):
        owner = lax.rem(me_p + q, n_inp)
        rows = pl.ds(pl.multiple_of(b * group, group), group)
        return remote(parts.at[pl.ds(owner * per_owner, per_owner), rows],
                      landed.at[q - 1, :, rows],
                      s_sems.at[q - 1], r_sems.at[q - 1], (me_o, owner))

    def products(b, slot, start, stop):
        pieces = []
        for n in range(start, stop, lanes):
            sums = []
            for k in range(group):
                inner = jnp.dot(slab[slot, k], turned[:, n:n + lanes],
                                preferred_element_type=jnp.float32)
                sums.append(jnp.sum(inner * chosen[:, n:n + lanes], axis=0, keepdims=True))
            pieces.append(jnp.concatenate(sums, axis=0))
        total = jnp.concatenate(pieces, axis=1)
        rows = pl.ds(pl.multiple_of(b * group, group), group)
        for s, (d, e) in enumerate(order):
            low, high = max(start, s * cells_own), min(stop, (s + 1) * cells_own)
            if low < high:
                parts[out_of(d, e), rows, low - s * cells_own:high - s * cells_own] = (
                    total[:, low - start:high - start])

    def finish(b, slot):
        for q in range(1, n_inp):
            send_part(b, q).start()

        @pl.when(b + slots < blocks)
        def _():
            fetch(b + slots, slot).start()

    turn(0, lanes)

    def lead(b, carry):
        for d in range(2, nz + 1):
            @pl.when(b == min((d - 1) * slots // max(nz - 1, 1), slots - 1))
            def _():
                if d < nz:
                    relay_z(d)
                relay_x(d - 1)
        fetch(b, b).wait()
        products(b, b, 0, lanes)
        return carry

    lax.fori_loop(0, slots, lead, 0)
    for d, e in order[early:]:
        core_copy(e, d).wait_recv()
    if lanes < cells:
        turn(lanes, cells)

    def follow(b, carry):
        if lanes < cells:
            products(b, b, lanes, cells)
        finish(b, b)
        return carry

    lax.fori_loop(0, slots, follow, 0)

    def whole(b, carry):
        slot = lax.rem(b, slots)
        fetch(b, slot).wait()
        products(b, slot, 0, cells)
        finish(b, slot)
        return carry

    if slots < blocks:
        lax.fori_loop(slots, blocks, whole, 0)

    everything = [remote(parts.at[pl.ds(0, per_owner)], landed.at[q - 1], s_sems.at[q - 1],
                         r_sems.at[q - 1], (me_o, lax.rem(me_p + q, n_inp))) for q in range(1, n_inp)]
    for d in range(1, nz):
        z_copy(d).wait_send()
    for d, e in order:
        if e > 0:
            x_copy(e, d).wait_send()
        if (d, e) != (0, 0):
            core_copy(e, d).wait_send()
    for copy in everything:
        copy.wait_recv()
    for s in range(per_owner):
        total = parts[me_p * per_owner + s]
        for q in range(1, n_inp):
            total = total + landed[q - 1, s]
        out[s * cells_own:(s + 1) * cells_own, :] = total.T[0:cells_own, :].astype(out.dtype)
    for copy in everything:
        copy.wait_send()


def solution(mesh):
    n_out, n_inp = mesh.shape["out"], mesh.shape["inp"]
    nx = len({device.coords[0] for device in mesh.devices[:, 0]})

    def local(tensor, state):
        rows_out, rows_inp, width = tensor.shape
        cells_own = state.shape[0]
        cells = n_out * cells_own
        per_owner = n_out // n_inp
        padded = -(-cells_own // 128) * 128
        nz = n_out // nx
        group = min(GROUP, rows_out)
        slots = min(SLOTS, rows_out // group)
        return pl.pallas_call(
            functools.partial(kernel, nx, n_out, n_inp),
            out_shape=jax.ShapeDtypeStruct((cells // n_inp, rows_out), jnp.bfloat16),
            in_specs=[pl.BlockSpec(memory_space=pl.ANY), pl.BlockSpec(memory_space=pltpu.VMEM)],
            out_specs=pl.BlockSpec(memory_space=pltpu.VMEM),
            scratch_shapes=[
                pltpu.VMEM((cells, width), jnp.bfloat16),
                pltpu.VMEM((width, cells), jnp.bfloat16),
                pltpu.VMEM((rows_inp, cells), jnp.float32),
                pltpu.VMEM((slots, group, rows_inp, width), jnp.bfloat16),
                pltpu.VMEM((n_out, rows_out, padded), jnp.float32),
                pltpu.VMEM((n_inp - 1, per_owner, rows_out, padded), jnp.float32),
                pltpu.SemaphoreType.DMA((2, nz)),
                pltpu.SemaphoreType.DMA((2, nx, nz)),
                pltpu.SemaphoreType.DMA((2, nx, nz)),
                pltpu.SemaphoreType.DMA((slots,)),
                pltpu.SemaphoreType.DMA((n_inp - 1,)),
                pltpu.SemaphoreType.DMA((n_inp - 1,)),
            ],
            compiler_params=pltpu.CompilerParams(
                collective_id=0, has_side_effects=True, vmem_limit_bytes=60 * 2**20),
            name="collide",
        )(tensor, state)

    return jax.shard_map(
        local, mesh=mesh, in_specs=(P("out", "inp", None), P("out", None)),
        out_specs=P("inp", "out"), check_vma=False)
```

profile of v0, /device:TPU:0, one launch (start us, length us, event | category | flops | bytes accessed | tf_op | source)
XLA Modules:
  0.0 76.2 jit_solution(16358831089135851923)
XLA Ops:
  0.0 74.7 %collide.1 = bf16[192,128]{1,0:T(8,128)(2,1)} custom-call(bf16[128,256,1024]{2,1,0:T(8,128)(2,1)} %tensor.1, bf16[96,1024]{1,0:T(8,128)(2,1)} %state.1), custom_call_target="tpu_custom_call" | custom-call | tf_op jit(solution)/shard_map/collide/pallas_call | solution.py:213
  74.7 1.4 %copy.4 = bf16[192,128]{1,0:T(8,128)(2,1)} copy(bf16[192,128]{1,0:T(8,128)(2,1)} %collide.1) | data formatting | bytes 98304
where the time goes:
time: 76.4 us; the launch traced here: 76.2 us
  Pallas kernels  74.7 us (98%)
  local copies, waits for them, and re-layouts  1.42 us (2%)
    pallas_call x1, Pallas kernels, local(): pl.pallas_call(functools.partial(kernel, nx, n_out, n_inp), out_shape=jax...  74.7 us

commit v1 on v0

--- a/solution.py
+++ b/solution.py
@@ -20,7 +20,7 @@
 
 
 def kernel(nx, n_out, n_inp, tensor, state, out, gathered, turned, chosen, slab, parts, landed,
-           z_sems, x_sems, core_sems, t_sems, s_sems, r_sems):
+           own_sem, z_sems, x_sems, core_sems, t_sems, s_sems, r_sems):
     rows_out, rows_inp, width = tensor.shape
     cells_own = state.shape[0]
     cells = n_out * cells_own
@@ -45,6 +45,8 @@
         return pltpu.make_async_copy(
             tensor.at[pl.ds(b * group, group)], slab.at[slot], t_sems.at[slot])
 
+    own_copy = pltpu.make_async_copy(state, gathered.at[pl.ds(0, cells_own)], own_sem)
+    own_copy.start()
     for b in range(slots):
         fetch(b, b).start()
 
@@ -94,7 +96,7 @@
         x_copy(e, 0).start()
     for d in range(1, nz):
         z_copy(d).start()
-    gathered[0:cells_own, :] = state[...]
+    own_copy.wait()
     relay_x(0)
     relay_z(1)
     order = [(d, e) for d in range(nz) for e in range(nx)]
@@ -212,8 +214,8 @@
         slots = min(SLOTS, rows_out // group)
         return pl.pallas_call(
             functools.partial(kernel, nx, n_out, n_inp),
-            out_shape=jax.ShapeDtypeStruct((cells // n_inp, rows_out), jnp.bfloat16),
-            in_specs=[pl.BlockSpec(memory_space=pl.ANY), pl.BlockSpec(memory_space=pltpu.VMEM)],
+            out_shape=pltpu.VMEM((cells // n_inp, rows_out), jnp.bfloat16),
+            in_specs=[pl.BlockSpec(memory_space=pl.ANY), pl.BlockSpec(memory_space=pl.ANY)],
             out_specs=pl.BlockSpec(memory_space=pltpu.VMEM),
             scratch_shapes=[
                 pltpu.VMEM((cells, width), jnp.bfloat16),
@@ -222,6 +224,7 @@
                 pltpu.VMEM((slots, group, rows_inp, width), jnp.bfloat16),
                 pltpu.VMEM((n_out, rows_out, padded), jnp.float32),
                 pltpu.VMEM((n_inp - 1, per_owner, rows_out, padded), jnp.float32),
+                pltpu.SemaphoreType.DMA,
                 pltpu.SemaphoreType.DMA((2, nz)),
                 pltpu.SemaphoreType.DMA((2, nx, nz)),
                 pltpu.SemaphoreType.DMA((2, nx, nz)),

time: 76.4 us -> 76.1 us (level)
  local copies, waits for them, and re-layouts: 1.42 us -> 0.62 us
    unnamed x1, local copies, waits for them, and re-layouts: 1.42 us -> 0.62 us
where the time goes in v1:
time: 76.1 us; the launch traced here: 75.9 us
  Pallas kernels  75.3 us (99%)
    pallas_call x1, Pallas kernels, local(): pl.pallas_call(functools.partial(kernel, nx, n_out, n_inp), out_shape=plt...  75.3 us

profile of v1, /device:TPU:0, one launch (start us, length us, event | category | flops | bytes accessed | tf_op | source)
XLA Modules:
  0.0 75.9 jit_solution(14087168824911447214)
XLA Ops:
  0.0 75.3 %collide.1 = bf16[192,128]{1,0:T(8,128)(2,1)S(1)} custom-call(bf16[128,256,1024]{2,1,0:T(8,128)(2,1)} %tensor.1, bf16[96,1024]{1,0:T(8,128)(2,1)} %state.1), custom_call_target="tpu_custom_call" | custom-call | tf_op jit(solution)/shard_map/collide/pallas_call | solution.py:215
  75.3 0.6 copy.4

commit v2 on v1

v2 whole, which is shorter than its diff:
```python
import functools

import jax
import jax.numpy as jnp
from jax import lax
from jax.experimental import pallas as pl
from jax.experimental.pallas import tpu as pltpu
from jax.sharding import PartitionSpec as P

MESH = pl.DeviceIdType.MESH
GROUP = 16
SLOTS = 6
LAST = 2
OWN = 2
NEAR = 3
HOOKS = (10, 12, 19, 36, 38, 62)
ROWS = (((1,), (1,)), ((), ()))


def flip(value, bits):
    for bit in (1 << n for n in range(bits.bit_length())):
        if bits & bit:
            value = value + bit * (1 - 2 * ((value // bit) % 2))
    return value


def differ(a, b, size):
    total = 0
    for bit in (1 << n for n in range((size - 1).bit_length())):
        total = total + bit * ((a // bit + b // bit) % 2)
    return total


def kernel(nx, n_out, n_inp, tensor, state, out, gathered, chosen, slab, parts, landed,
           own_sem, z_sems, x_sems, core_sems, t_sems, s_sems, r_sems):
    rows_out, rows_inp, width = tensor.shape
    cells_own = state.shape[0]
    cells = n_out * cells_own
    nz = n_out // nx
    per_owner = n_out // n_inp
    slots, group = slab.shape[0], slab.shape[1]
    blocks = rows_out // group
    own = min(OWN, slots - 1)
    near = min(NEAR, n_out)
    halves = 2
    half_width = width // halves

    me_o = lax.axis_index("out")
    me_p = lax.axis_index("inp")
    z, x = me_o // nx, me_o % nx
    half = me_p % halves
    partner = me_p + 1 - 2 * half
    cols = pl.ds(pl.multiple_of(half * half_width, 128), half_width)

    def fetch(b, slot):
        return pltpu.make_async_copy(
            tensor.at[pl.ds(b * group, group)], slab.at[slot], t_sems.at[slot])

    own_copy = pltpu.make_async_copy(state, gathered.at[pl.ds(0, cells_own)], own_sem)
    own_copy.start()
    for b in range(min(2, slots)):
        fetch(b, b).start()

    def out_of(d, e):
        return flip(z, d) * nx + flip(x, e)

    barrier = pltpu.get_barrier_semaphore()
    peers = [(out_of(d, 0), me_p) for d in range(1, nz)]
    peers += [(out_of(0, e), me_p) for e in range(1, nx)]
    peers += [(me_o, lax.rem(me_p + q, n_inp)) for q in range(1, n_inp)]
    for device in peers:
        pl.semaphore_signal(barrier, inc=1, device_id=device, device_id_type=MESH)

    def remote(src, dst, send, recv, device):
        return pltpu.make_async_remote_copy(
            src_ref=src, dst_ref=dst, send_sem=send, recv_sem=recv,
            device_id=device, device_id_type=MESH)

    def shard(d, e):
        return gathered.at[pl.ds((d * nx + e) * cells_own, cells_own), cols]

    def z_copy(d):
        return remote(state.at[:, cols], shard(d, 0), z_sems.at[0, d], z_sems.at[1, d],
                      (out_of(d, 0), me_p))

    def x_copy(e, d):
        return remote(state.at[:, cols] if d == 0 else shard(d, 0), shard(d, e),
                      x_sems.at[0, e, d], x_sems.at[1, e, d], (out_of(0, e), me_p))

    def core_copy(e, d):
        return remote(shard(d, e), shard(d, e), core_sems.at[0, e, d], core_sems.at[1, e, d],
                      (me_o, partner))

    def relay_x(d):
        for e in range(1, nx):
            x_copy(e, d).wait_recv()
            core_copy(e, d).start()

    def relay_z(d):
        z_copy(d).wait_recv()
        for e in range(1, nx):
            x_copy(e, d).start()
        core_copy(0, d).start()

    wide = max(rows_inp, 128)
    first = pl.multiple_of(me_p * rows_inp // wide * wide, wide)

    def choose(start, stop):
        block = gathered[start:stop, pl.ds(first, wide)].astype(jnp.float32)
        piece = block[:, 0:rows_inp]
        for n in range(1, wide // rows_inp):
            piece = jnp.where(me_p % (wide // rows_inp) == n,
                              block[:, n * rows_inp:(n + 1) * rows_inp], piece)
        chosen[start:stop, :] = piece

    def visit(b, slot, start, size, hooks=()):
        rows = pl.ds(start, size)
        lane = lax.broadcasted_iota(jnp.int32, (size, rows_out), 1)
        kept = parts[rows, :]
        for k in range(group):
            for at, act in hooks:
                if at * group // 16 == k:
                    act()
            inner = lax.dot_general(gathered[rows, :], slab[slot, k], ROWS,
                                    preferred_element_type=jnp.float32)
            sums = jnp.sum(inner * chosen[rows, :], axis=1, keepdims=True)
            kept = jnp.where(lane == b * group + k, sums, kept)
        parts[rows, :] = kept

    parts[...] = jnp.zeros_like(parts)
    own_copy.wait()
    choose(0, cells_own)
    pl.semaphore_wait(barrier, len(peers))
    for e in range(1, nx):
        x_copy(e, 0).start()
    for d in range(1, nz):
        z_copy(d).start()

    hooks = [[] for _ in range(slots)]

    def hook(b, at, act):
        hooks[min(b, slots - 1)].append((at, act))

    hook(own - 1, HOOKS[0], lambda: (relay_x(0), relay_z(1)))
    for d in range(2, nz):
        place = HOOKS[min(2 * d - 3, 3)]
        hook(own + place // 16, place % 16, lambda d=d: relay_z(d))
        place = HOOKS[min(2 * d - 2, 4)]
        hook(own + place // 16, place % 16, lambda d=d: relay_x(d - 1))
    hook(own + HOOKS[5] // 16, HOOKS[5] % 16, lambda: relay_x(nz - 1))

    order = [(d, e) for d in range(nz) for e in range(nx)]
    for b in range(slots):
        if b == own:
            for d, e in order[1:near]:
                core_copy(e, d).wait_recv()
            choose(cells_own, near * cells_own)
        fetch(b, b).wait()
        if b + 2 < slots:
            fetch(b + 2, b + 2).start()
        visit(b, b, 0, (1 if b < own else near) * cells_own, hooks[b])
    for d, e in order[near:]:
        core_copy(e, d).wait_recv()
    choose(near * cells_own, cells)

    def refill(b):
        @pl.when(b + slots < blocks)
        def _():
            fetch(b + slots, b).start()

    def most(b, carry):
        visit(b, b, cells_own, cells - cells_own)
        refill(b)
        return carry

    lax.fori_loop(0, own, most, 0)

    def rest(b, carry):
        visit(b, b, near * cells_own, cells - near * cells_own)
        refill(b)
        return carry

    lax.fori_loop(own, slots, rest, 0)

    count = n_out // 2
    span = count * cells_own
    mine = 1 - differ(z // max(nz // 2, 1), me_p // max(n_inp // 2, 1), 2)
    last = blocks - slots

    def sends(side, act):
        for s in range(count):
            zone = flip(z, s // nx)
            zone = zone + side * (nz // 2) * (1 - 2 * ((zone // (nz // 2)) % 2))
            target = zone * nx + flip(x, s % nx)
            owner, place = target // per_owner, target % per_owner

            @pl.when(owner != me_p)
            def _():
                q = lax.rem(owner - me_p + n_inp, n_inp)
                act(remote(
                    parts.at[pl.ds(pl.multiple_of(side * span, 32) + s * cells_own, cells_own)],
                    landed.at[q - 1, place], s_sems.at[q - 1, place], r_sems.at[q - 1, place],
                    (me_o, owner)))

    def finish(t, carry):
        side = differ(t // last, mine, 2)
        b = slots + t % last

        @pl.when(t < last)
        def _():
            fetch(b, b - slots).wait()

        @pl.when(t == last)
        def _():
            sends(mine, lambda copy: copy.start())

        visit(b, b - slots, pl.multiple_of(side * span, 32), span)
        return carry

    lax.fori_loop(0, 2 * last, finish, 0)
    sends(1 - mine, lambda copy: copy.start())

    for d in range(1, nz):
        z_copy(d).wait_send()
    for d, e in order:
        if e > 0:
            x_copy(e, d).wait_send()
        if (d, e) != (0, 0):
            core_copy(e, d).wait_send()
    for s in range(per_owner):
        target = me_p * per_owner + s
        slot = differ(z, target // nx, nz) * nx + differ(x, target % nx, nx)
        total = parts[pl.ds(pl.multiple_of(slot * cells_own, cells_own), cells_own), :]
        for q in range(1, n_inp):
            remote(landed.at[q - 1, s], landed.at[q - 1, s], s_sems.at[q - 1, s],
                   r_sems.at[q - 1, s], (me_o, partner)).wait_recv()
            total = total + landed[q - 1, s]
        out[s * cells_own:(s + 1) * cells_own, :] = total.astype(out.dtype)
    sends(mine, lambda copy: copy.wait_send())
    sends(1 - mine, lambda copy: copy.wait_send())


def solution(mesh):
    n_out, n_inp = mesh.shape["out"], mesh.shape["inp"]
    nx = len({device.coords[0] for device in mesh.devices[:, 0]})

    def local(tensor, state):
        rows_out, rows_inp, width = tensor.shape
        cells_own = state.shape[0]
        cells = n_out * cells_own
        per_owner = n_out // n_inp
        nz = n_out // nx
        group = min(GROUP, rows_out // 4)
        slots = min(SLOTS, rows_out // group - LAST)
        return pl.pallas_call(
            functools.partial(kernel, nx, n_out, n_inp),
            out_shape=pltpu.VMEM((cells // n_inp, rows_out), jnp.bfloat16),
            in_specs=[pl.BlockSpec(memory_space=pl.ANY), pl.BlockSpec(memory_space=pl.ANY)],
            out_specs=pl.BlockSpec(memory_space=pltpu.VMEM),
            scratch_shapes=[
                pltpu.VMEM((cells, width), jnp.bfloat16),
                pltpu.VMEM((cells, rows_inp), jnp.float32),
                pltpu.VMEM((slots, group, rows_inp, width), jnp.bfloat16),
                pltpu.VMEM((cells, rows_out), jnp.float32),
                pltpu.VMEM((n_inp - 1, per_owner, cells_own, rows_out), jnp.float32),
                pltpu.SemaphoreType.DMA,
                pltpu.SemaphoreType.DMA((2, nz)),
                pltpu.SemaphoreType.DMA((2, nx, nz)),
                pltpu.SemaphoreType.DMA((2, nx, nz)),
                pltpu.SemaphoreType.DMA((slots,)),
                pltpu.SemaphoreType.DMA((n_inp - 1, per_owner)),
                pltpu.SemaphoreType.DMA((n_inp - 1, per_owner)),
            ],
            compiler_params=pltpu.CompilerParams(
                collective_id=0, has_side_effects=True, vmem_limit_bytes=60 * 2**20),
            name="collide",
        )(tensor, state)

    return jax.shard_map(
        local, mesh=mesh, in_specs=(P("out", "inp", None), P("out", None)),
        out_specs=P("inp", "out"), check_vma=False)
```

time: 76.1 us -> 71.9 us (0.945)
  Pallas kernels: 75.3 us -> 71.1 us
    pallas_call x1, Pallas kernels: 75.3 us -> 71.1 us  [local(): pl.pallas_call(functools.partial(kernel, nx, n_out, n_inp), out_shape=plt...]
where the time goes in v2:
time: 71.9 us; the launch traced here: 71.7 us
  Pallas kernels  71.1 us (99%)
    pallas_call x1, Pallas kernels, local(): pl.pallas_call(functools.partial(kernel, nx, n_out, n_inp), out_shape=plt...  71.1 us

profile of v2, /device:TPU:0, one launch (start us, length us, event | category | flops | bytes accessed | tf_op | source)
XLA Modules:
  0.0 71.7 jit_solution(17982520914273520146)
XLA Ops:
  0.0 71.1 %collide.1 = bf16[192,128]{1,0:T(8,128)(2,1)S(1)} custom-call(bf16[128,256,1024]{2,1,0:T(8,128)(2,1)} %tensor.1, bf16[96,1024]{1,0:T(8,128)(2,1)} %state.1), custom_call_target="tpu_custom_call" | custom-call | tf_op jit(solution)/shard_map/collide/pallas_call | solution.py:255
  71.1 0.6 copy.4

commit v3 on v2

--- a/solution.py
+++ b/solution.py
@@ -13,7 +13,7 @@
 LAST = 2
 OWN = 2
 NEAR = 3
-HOOKS = (10, 12, 19, 36, 38, 62)
+HOOKS = (8, 10, 16, 24, 32, 48)
 ROWS = (((1,), (1,)), ((), ()))
 
 
@@ -58,8 +58,7 @@
 
     own_copy = pltpu.make_async_copy(state, gathered.at[pl.ds(0, cells_own)], own_sem)
     own_copy.start()
-    for b in range(min(2, slots)):
-        fetch(b, b).start()
+    fetch(0, 0).start()
 
     def out_of(d, e):
         return flip(z, d) * nx + flip(x, e)
@@ -135,6 +134,7 @@
         x_copy(e, 0).start()
     for d in range(1, nz):
         z_copy(d).start()
+    fetch(1, 1).start()
 
     hooks = [[] for _ in range(slots)]
 

time: 71.9 us -> 69.8 us (0.971)
  Pallas kernels: 71.1 us -> 69 us
    pallas_call x1, Pallas kernels: 71.1 us -> 69 us  [local(): pl.pallas_call(functools.partial(kernel, nx, n_out, n_inp), out_shape=plt...]
where the time goes in v3:
time: 69.8 us; the launch traced here: 69.6 us
  Pallas kernels  69 us (99%)
    pallas_call x1, Pallas kernels, local(): pl.pallas_call(functools.partial(kernel, nx, n_out, n_inp), out_shape=plt...  69 us

profile of v3, /device:TPU:0, one launch (start us, length us, event | category | flops | bytes accessed | tf_op | source)
XLA Modules:
  0.0 69.6 jit_solution(14881675721786764294)
XLA Ops:
  0.0 69.0 %collide.1 = bf16[192,128]{1,0:T(8,128)(2,1)S(1)} custom-call(bf16[128,256,1024]{2,1,0:T(8,128)(2,1)} %tensor.1, bf16[96,1024]{1,0:T(8,128)(2,1)} %state.1), custom_call_target="tpu_custom_call" | custom-call | tf_op jit(solution)/shard_map/collide/pallas_call | solution.py:255
  69.0 0.6 copy.4

commit v4 on v3

--- a/solution.py
+++ b/solution.py
@@ -175,17 +175,21 @@
 
     lax.fori_loop(0, own, most, 0)
 
-    def rest(b, carry):
-        visit(b, b, near * cells_own, cells - near * cells_own)
-        refill(b)
+    pair = 2 if (slots - own) % 2 == 0 else 1
+
+    def rest(i, carry):
+        for n in range(pair):
+            b = own + i * pair + n
+            visit(b, b, near * cells_own, cells - near * cells_own)
+        for n in range(pair):
+            refill(own + i * pair + n)
         return carry
 
-    lax.fori_loop(own, slots, rest, 0)
+    lax.fori_loop(0, (slots - own) // pair, rest, 0)
 
     count = n_out // 2
     span = count * cells_own
     mine = 1 - differ(z // max(nz // 2, 1), me_p // max(n_inp // 2, 1), 2)
-    last = blocks - slots
 
     def sends(side, act):
         for s in range(count):
@@ -203,21 +207,19 @@
                     (me_o, owner)))
 
     def finish(t, carry):
-        side = differ(t // last, mine, 2)
-        b = slots + t % last
-
-        @pl.when(t < last)
-        def _():
-            fetch(b, b - slots).wait()
-
-        @pl.when(t == last)
+        side = differ(t, mine, 2)
+
+        @pl.when(t == 1)
         def _():
             sends(mine, lambda copy: copy.start())
 
-        visit(b, b - slots, pl.multiple_of(side * span, 32), span)
+        for b in range(slots, blocks):
+            visit(b, b - slots, pl.multiple_of(side * span, 32), span)
         return carry
 
-    lax.fori_loop(0, 2 * last, finish, 0)
+    for b in range(slots, blocks):
+        fetch(b, b - slots).wait()
+    lax.fori_loop(0, 2, finish, 0)
     sends(1 - mine, lambda copy: copy.start())
 
     for d in range(1, nz):

time: 69.8 us -> 69 us (0.989)
  Pallas kernels: 69 us -> 68.2 us
    pallas_call x1, Pallas kernels: 69 us -> 68.2 us  [local(): pl.pallas_call(functools.partial(kernel, nx, n_out, n_inp), out_shape=plt...]
where the time goes in v4:
time: 69 us; the launch traced here: 68.8 us
  Pallas kernels  68.2 us (99%)
    pallas_call x1, Pallas kernels, local(): pl.pallas_call(functools.partial(kernel, nx, n_out, n_inp), out_shape=plt...  68.2 us

profile of v4, /device:TPU:0, one launch (start us, length us, event | category | flops | bytes accessed | tf_op | source)
XLA Modules:
  0.0 68.8 jit_solution(10670090354423054670)
XLA Ops:
  0.0 68.2 %collide.1 = bf16[192,128]{1,0:T(8,128)(2,1)S(1)} custom-call(bf16[128,256,1024]{2,1,0:T(8,128)(2,1)} %tensor.1, bf16[96,1024]{1,0:T(8,128)(2,1)} %state.1), custom_call_target="tpu_custom_call" | custom-call | tf_op jit(solution)/shard_map/collide/pallas_call | solution.py:257
  68.2 0.6 copy.4

commit v5 on v4

--- a/solution.py
+++ b/solution.py
@@ -127,14 +127,14 @@
         parts[rows, :] = kept
 
     parts[...] = jnp.zeros_like(parts)
-    own_copy.wait()
-    choose(0, cells_own)
     pl.semaphore_wait(barrier, len(peers))
     for e in range(1, nx):
         x_copy(e, 0).start()
     for d in range(1, nz):
         z_copy(d).start()
     fetch(1, 1).start()
+    own_copy.wait()
+    choose(0, cells_own)
 
     hooks = [[] for _ in range(slots)]
 

time: 69 us -> 69 us (level)
  no operation moved by 1% of the time
where the time goes in v5:
time: 69 us; the launch traced here: 68.8 us
  Pallas kernels  68.2 us (99%)
    pallas_call x1, Pallas kernels, local(): pl.pallas_call(functools.partial(kernel, nx, n_out, n_inp), out_shape=plt...  68.2 us

profile of v5, /device:TPU:0, one launch (start us, length us, event | category | flops | bytes accessed | tf_op | source)
XLA Modules:
  0.0 68.8 jit_solution(13136164515256592301)
XLA Ops:
  0.0 68.2 %collide.1 = bf16[192,128]{1,0:T(8,128)(2,1)S(1)} custom-call(bf16[128,256,1024]{2,1,0:T(8,128)(2,1)} %tensor.1, bf16[96,1024]{1,0:T(8,128)(2,1)} %state.1), custom_call_target="tpu_custom_call" | custom-call | tf_op jit(solution)/shard_map/collide/pallas_call | solution.py:257
  68.2 0.6 copy.4

commit v6 on v5

--- a/solution.py
+++ b/solution.py
@@ -13,7 +13,7 @@
 LAST = 2
 OWN = 2
 NEAR = 3
-HOOKS = (8, 10, 16, 24, 32, 48)
+HOOKS = (8, 9, 15, 24, 30, 46)
 ROWS = (((1,), (1,)), ((), ()))
 
 

time: 69 us -> 70.1 us (1.016)
  Pallas kernels: 68.2 us -> 69.3 us
    pallas_call x1, Pallas kernels: 68.2 us -> 69.3 us  [local(): pl.pallas_call(functools.partial(kernel, nx, n_out, n_inp), out_shape=plt...]
where the time goes in v6:
time: 70.1 us; the launch traced here: 70 us
  Pallas kernels  69.3 us (99%)
    pallas_call x1, Pallas kernels, local(): pl.pallas_call(functools.partial(kernel, nx, n_out, n_inp), out_shape=plt...  69.3 us

profile of v6, /device:TPU:0, one launch (start us, length us, event | category | flops | bytes accessed | tf_op | source)
XLA Modules:
  0.0 70.0 jit_solution(14035195554421729335)
XLA Ops:
  0.0 69.3 %collide.1 = bf16[192,128]{1,0:T(8,128)(2,1)S(1)} custom-call(bf16[128,256,1024]{2,1,0:T(8,128)(2,1)} %tensor.1, bf16[96,1024]{1,0:T(8,128)(2,1)} %state.1), custom_call_target="tpu_custom_call" | custom-call | tf_op jit(solution)/shard_map/collide/pallas_call | solution.py:257
  69.3 0.6 copy.4
